TPU v7x, 32 devices: a whole 2x2x4 slice. The times are simulated.
32 devices in a mesh: curve: 8 (over z, x), level: 4 (over y, core).
Axes of the slice: x: 2, y: 2, z: 4, core: 2. Of those that a mesh axis runs over, the one named last changes fastest.
Arguments:
- right_side: float32 [512, 4096], P(None, ('curve', 'level')), may hold values from -6 to 6
- counts: int32 [32], replicated, may hold values from 96 to 128, as said below
- neighbours: int32 [6, 4096], P(None, ('curve', 'level')), may hold values from -1 to 4095, as said below
Outputs:
- solution: float32 [512, 4096], P(None, ('curve', 'level'))
- residual: float32 [512, 4096], P(None, ('curve', 'level'))
- residual_norm: float32 [], replicated
Inputs may be any that keep to these rules, and one draw needn't show every extreme that they name: `counts`: some device holds 128 live bricks and some device holds 96. `neighbours`: A slot's global number is its device times 128 plus its position. The relation is symmetric across opposite faces; padding slots have -1 on every face and no brick names them. Live bricks are numbered along the curve; the brick across face 0, 2 or 4 lies earlier on the curve and the one across face 1, 3 or 5 later, at most 256 live bricks away.
All inputs are finite; a program needn't handle non-finite values.
Results may differ from a plain program's by a relative error of at most 0.00027.
Values sent between devices are 32-bit elements; how exact they have to be, the bound alone decides.
A program may use at most 64 MiB of HBM per device.

v0:
```python
import jax
import jax.numpy as jnp
from jax import lax
from jax.sharding import PartitionSpec as P

MIN_LIVE = 96
LAYER = 256
HOPS = 3
OPPOSITE = (1, 0, 3, 2, 5, 4)
RELAXATION = 2.0 / 3.0


def from_behind(block, axis, distance):
    devices = range(lax.axis_size(axis))
    route = [(i - distance, i) for i in devices if i - distance in devices]
    return lax.ppermute(block, axis, route)


def brick_faces(values, extent):
    volume = values.reshape(extent, extent, extent, -1)
    surfaces = [
        volume[0],
        volume[extent - 1],
        volume[:, 0],
        volume[:, extent - 1],
        volume[:, :, 0],
        volume[:, :, extent - 1],
    ]
    return jnp.stack([one_face.reshape(extent * extent, -1) for one_face in surfaces])


def apply_operator(values, ghosts, extent, weight):
    brick_count = values.shape[1]
    volume = values.reshape(extent, extent, extent, brick_count)
    padded = jnp.pad(volume, ((1, 1), (1, 1), (1, 1), (0, 0)))
    shaped = [ghost.reshape(extent, extent, brick_count) for ghost in ghosts]
    padded = padded.at[0, 1:-1, 1:-1].set(shaped[0])
    padded = padded.at[-1, 1:-1, 1:-1].set(shaped[1])
    padded = padded.at[1:-1, 0, 1:-1].set(shaped[2])
    padded = padded.at[1:-1, -1, 1:-1].set(shaped[3])
    padded = padded.at[1:-1, 1:-1, 0].set(shaped[4])
    padded = padded.at[1:-1, 1:-1, -1].set(shaped[5])
    beside = padded[2:, 1:-1, 1:-1] + padded[:-2, 1:-1, 1:-1]
    beside = beside + padded[1:-1, 2:, 1:-1] + padded[1:-1, :-2, 1:-1]
    beside = beside + padded[1:-1, 1:-1, 2:] + padded[1:-1, 1:-1, :-2]
    return ((6.0 * volume - beside) * weight).reshape(extent * extent * extent, brick_count)


def restrict(values):
    brick_count = values.shape[1]
    grouped = values.reshape(4, 2, 4, 2, 4, 2, brick_count)
    return jnp.mean(grouped, axis=(1, 3, 5)).reshape(64, brick_count)


def prolong(coarse):
    brick_count = coarse.shape[1]
    spread = jnp.broadcast_to(
        coarse.reshape(4, 1, 4, 1, 4, 1, brick_count), (4, 2, 4, 2, 4, 2, brick_count)
    )
    return spread.reshape(512, brick_count)


def precondition(residual_in, exchange):
    relax_fine = RELAXATION / 6.0
    relax_coarse = RELAXATION / 1.5
    sweep_one = relax_fine * residual_in
    sweep_two = sweep_one + relax_fine * (
        residual_in - apply_operator(sweep_one, exchange(brick_faces(sweep_one, 8)), 8, 1.0)
    )
    defect = residual_in - apply_operator(sweep_two, exchange(brick_faces(sweep_two, 8)), 8, 1.0)
    coarse_rhs = restrict(defect)
    coarse_one = relax_coarse * coarse_rhs
    coarse_two = coarse_one + relax_coarse * (
        coarse_rhs - apply_operator(coarse_one, exchange(brick_faces(coarse_one, 4)), 4, 0.25)
    )
    sweep_three = sweep_two + prolong(coarse_two)
    return sweep_three + relax_fine * (
        residual_in - apply_operator(sweep_three, exchange(brick_faces(sweep_three, 8)), 8, 1.0)
    )


def local(right_side, counts, neighbours):
    slot_count = right_side.shape[1]
    device = lax.axis_index(("curve", "level"))
    own_count = counts[device]
    live_slot = jnp.arange(slot_count, dtype=jnp.int32) < own_count
    residual_in = jnp.where(live_slot[None, :], right_side, jnp.zeros_like(right_side))
    widths = [min(slot_count, LAYER - (hop - 1) * MIN_LIVE) for hop in range(1, HOPS + 1)]
    window_starts = []
    running = slot_count
    for width in widths:
        window_starts.append(running)
        running = running + width
    width_table = jnp.array(widths, dtype=jnp.int32)
    start_table = jnp.array(window_starts, dtype=jnp.int32)
    present = neighbours >= 0
    safe_slot = jnp.where(present, neighbours, 0)
    owner = safe_slot // slot_count
    offset = safe_slot % slot_count
    earlier = (jnp.arange(6, dtype=jnp.int32) % 2 == 0)[:, None]
    hop_index = jnp.clip(jnp.where(earlier, device - owner, owner - device), 1, HOPS) - 1
    skipped = jnp.where(earlier, jnp.maximum(counts[owner] - width_table[hop_index], 0), 0)
    position = jnp.where(owner == device, offset, start_table[hop_index] + offset - skipped)
    position = jnp.clip(jnp.where(present, position, 0), 0, running - 1)

    def exchange(surface):
        odd_faces = surface[1::2]
        even_faces = surface[0::2]
        lower = []
        upper = []
        for hop in range(1, HOPS + 1):
            width = widths[hop - 1]
            piece = lax.dynamic_slice_in_dim(odd_faces, jnp.maximum(own_count - width, 0), width, 2)
            lower.append(from_behind(piece, ("curve", "level"), hop))
            upper.append(from_behind(even_faces[:, :, :width], ("curve", "level"), -hop))
        ghosts = []
        for face_id in range(6):
            windows = lower if face_id % 2 == 0 else upper
            lookup = jnp.concatenate(
                [surface[OPPOSITE[face_id]]] + [window[face_id // 2] for window in windows], axis=1
            )
            picked = jnp.take(lookup, position[face_id], axis=1)
            ghosts.append(jnp.where(present[face_id][None, :], picked, jnp.zeros_like(picked)))
        return ghosts

    preconditioned = precondition(residual_in, exchange)
    image = apply_operator(preconditioned, exchange(brick_faces(preconditioned, 8)), 8, 1.0)
    local_along = jnp.sum(residual_in * preconditioned)
    local_curvature = jnp.sum(preconditioned * image)
    along, curvature, old_square, cross_term, image_square = lax.psum(
        (
            local_along,
            local_curvature,
            jnp.sum(residual_in * residual_in),
            jnp.sum(residual_in * image),
            jnp.sum(image * image),
        ),
        ("curve", "level"),
    )
    step_size = along / curvature
    solution = step_size * preconditioned
    residual = residual_in - step_size * image
    norm_square = old_square - 2.0 * step_size * cross_term + step_size * step_size * image_square
    return (solution, residual, jnp.sqrt(norm_square))


def solution(mesh):
    in_specs = (P(None, ("curve", "level")), P(), P(None, ("curve", "level")))
    out_specs = (P(None, ("curve", "level")), P(None, ("curve", "level")), P())
    return jax.shard_map(local, mesh=mesh, in_specs=in_specs, out_specs=out_specs, check_vma=False)
```

profile of v0, /device:TPU:0, one launch (start us, length us, event | category | flops | bytes accessed | tf_op | source)
XLA Modules:
  0.0 247.6 jit_solution(9839667775032948823)
XLA Ops:
  2.5 1.1 copy.169
  4.5 1.3 collective-permute-start.4
  5.8 1.3 collective-permute-start.3
  7.1 6.2 %collective-permute-start.1 = (f32[3,64,128]{1,2,0:T(8,128)S(1)}, f32[3,64,128]{1,2,0:T(8,128)S(1)}, u32[]{:S(2)}, u32[]{:S(2)}) collective-permute-start(f32[3,64,128]{1,2,0:T(8,128)S(1)} %get-tuple-element.404), channel_id=1, source_target_pairs={{0,2},{1,3},{2,4},{3,5},{4,6},{5,7},{6,8},{7,9},{8,10},{9,11},{10,... | collective-permute-start | bytes 294920 | tf_op jit(solution)/shard_map/ppermute | solution.py:16
  13.3 2.1 collective-permute-start
  16.1 5.5 %collective-permute-start.2 = (f32[3,64,64]{1,2,0:T(8,128)S(1)}, f32[3,64,64]{1,2,0:T(8,128)S(1)}, u32[]{:S(2)}, u32[]{:S(2)}) collective-permute-start(f32[3,64,64]{1,2,0:T(8,128)S(1)} %constant_dynamic-slice_fusion.4), channel_id=1, source_target_pairs={{0,3},{1,4},{2,5},{3,6},{4,7},{5,8},{6,9},{7,10},{8,11},{9,12},{10... | collective-permute-start | bytes 147464 | tf_op jit(solution)/shard_map/ppermute | solution.py:16
  23.0 4.8 %gather_fusion.1 = s32[768]{0:T(1024)S(1)} fusion(s32[32]{0:T(128)S(1)} %copy-done, s32[1024]{0:T(1024)S(1)} %get-tuple-element.555), kind=kCustom, calls=%fused_computation.31 | custom fusion | bytes 9216 | tf_op jit(solution)/shard_map/gather | solution.py:102
  28.5 4.8 %gather_fusion.2 = s32[768]{0:T(1024)S(1)} fusion(s32[3]{0:T(128)S(1)} %copy-done.2, s32[1024]{0:T(1024)S(1)} %get-tuple-element.556), kind=kCustom, calls=%fused_computation.32 | custom fusion | bytes 9216 | tf_op jit(solution)/shard_map/gather | solution.py:102
  33.3 4.8 %gather_fusion = s32[768]{0:T(1024)S(1)} fusion(s32[3]{0:T(128)S(1)} %copy-done.1, s32[1024]{0:T(1024)S(1)} %get-tuple-element.556), kind=kCustom, calls=%fused_computation.30 | custom fusion | bytes 9216 | tf_op jit(solution)/shard_map/gather | solution.py:103
  42.8 1.3 collective-permute-start.5
  44.1 4.6 %collective-permute-done.5 = f32[3,64,64]{1,2,0:T(8,128)S(1)} collective-permute-done((f32[3,64,64]{1,2,0:T(8,128)S(1)}, f32[3,64,64]{1,2,0:T(8,128)S(1)}, u32[]{:S(2)}, u32[]{:S(2)}) %collective-permute-start.5) | collective-permute-done | bytes 49184 | tf_op jit(solution)/shard_map/ppermute | solution.py:16
  56.3 0.8 gather_fusion.5
  60.4 3.3 %collective-permute-start.8 = (f32[3,64,64]{1,2,0:T(8,128)S(1)}, f32[3,64,64]{1,2,0:T(8,128)S(1)}, u32[]{:S(2)}, u32[]{:S(2)}) collective-permute-start(f32[3,64,64]{1,2,0:T(8,128)S(1)} %constant_dynamic-slice_fusion.3), channel_id=1, source_target_pairs={{0,3},{1,4},{2,5},{3,6},{4,7},{5,8},{6,9},{7,10},{8,11},{9,12},{10... | collective-permute-start | bytes 147464 | tf_op jit(solution)/shard_map/ppermute | solution.py:16
  63.8 1.3 collective-permute-start.10
  65.1 1.3 collective-permute-start.9
  66.4 5.4 %collective-permute-start.7 = (f32[3,64,128]{1,2,0:T(8,128)S(1)}, f32[3,64,128]{1,2,0:T(8,128)S(1)}, u32[]{:S(2)}, u32[]{:S(2)}) collective-permute-start(f32[3,64,128]{1,2,0:T(8,128)S(1)} %get-tuple-element.402), channel_id=1, source_target_pairs={{0,2},{1,3},{2,4},{3,5},{4,6},{5,7},{6,8},{7,9},{8,10},{9,11},{10,... | collective-permute-start | bytes 294920 | tf_op jit(solution)/shard_map/ppermute | solution.py:16
  71.8 3.3 %collective-permute-start.6 = (f32[3,64,128]{1,2,0:T(8,128)S(1)}, f32[3,64,128]{1,2,0:T(8,128)S(1)}, u32[]{:S(2)}, u32[]{:S(2)}) collective-permute-start(f32[3,64,128]{1,2,0:T(8,128)S(1)} %get-tuple-element.402), channel_id=1, source_target_pairs={{0,1},{1,2},{2,3},{3,4},{4,5},{5,6},{6,7},{7,8},{8,9},{9,10},{10,1... | collective-permute-start | bytes 294920 | tf_op jit(solution)/shard_map/ppermute | solution.py:16
  75.6 1.3 collective-permute-start.11
  77.6 6.5 %collective-permute-done.11 = f32[3,64,64]{1,2,0:T(8,128)S(1)} collective-permute-done((f32[3,64,64]{1,2,0:T(8,128)S(1)}, f32[3,64,64]{1,2,0:T(8,128)S(1)}, u32[]{:S(2)}, u32[]{:S(2)}) %collective-permute-start.11) | collective-permute-done | bytes 49184 | tf_op jit(solution)/shard_map/ppermute | solution.py:16
  84.8 0.9 gather_fusion.14
  97.2 3.9 %collective-permute-start.14 = (f32[3,16,64]{2,1,0:T(8,128)S(1)}, f32[3,16,64]{2,1,0:T(8,128)S(1)}, u32[]{:S(2)}, u32[]{:S(2)}) collective-permute-start(f32[3,16,64]{2,1,0:T(8,128)S(1)} %constant_dynamic-slice_fusion.2), channel_id=1, source_target_pairs={{0,3},{1,4},{2,5},{3,6},{4,7},{5,8},{6,9},{7,10},{8,11},{9,12},{10... | collective-permute-start | bytes 36872 | tf_op jit(solution)/shard_map/ppermute | solution.py:16
  101.1 1.3 collective-permute-start.16
  102.4 1.3 collective-permute-start.15
  103.7 6.0 %collective-permute-start.13 = (f32[3,16,128]{2,1,0:T(8,128)S(1)}, f32[3,16,128]{2,1,0:T(8,128)S(1)}, u32[]{:S(2)}, u32[]{:S(2)}) collective-permute-start(f32[3,16,128]{2,1,0:T(8,128)S(1)} %get-tuple-element.510), channel_id=1, source_target_pairs={{0,2},{1,3},{2,4},{3,5},{4,6},{5,7},{6,8},{7,9},{8,10},{9,11},{10,... | collective-permute-start | bytes 73736 | tf_op jit(solution)/shard_map/ppermute | solution.py:16
  109.7 2.1 collective-permute-start.12
  111.9 1.3 collective-permute-start.17
  113.2 5.7 %collective-permute-done.17 = f32[3,16,64]{2,1,0:T(8,128)S(1)} collective-permute-done((f32[3,16,64]{2,1,0:T(8,128)S(1)}, f32[3,16,64]{2,1,0:T(8,128)S(1)}, u32[]{:S(2)}, u32[]{:S(2)}) %collective-permute-start.17) | collective-permute-done | bytes 12320 | tf_op jit(solution)/shard_map/ppermute | solution.py:16
  123.5 0.8 gather_fusion.18
  127.3 3.9 %collective-permute-start.20 = (f32[3,64,64]{1,2,0:T(8,128)S(1)}, f32[3,64,64]{1,2,0:T(8,128)S(1)}, u32[]{:S(2)}, u32[]{:S(2)}) collective-permute-start(f32[3,64,64]{1,2,0:T(8,128)S(1)} %constant_dynamic-slice_fusion.1), channel_id=1, source_target_pairs={{0,3},{1,4},{2,5},{3,6},{4,7},{5,8},{6,9},{7,10},{8,11},{9,12},{10... | collective-permute-start | bytes 147464 | tf_op jit(solution)/shard_map/ppermute | solution.py:16
  131.3 1.3 collective-permute-start.22
  132.6 1.3 collective-permute-start.21
  133.9 6.2 %collective-permute-start.19 = (f32[3,64,128]{1,2,0:T(8,128)S(1)}, f32[3,64,128]{1,2,0:T(8,128)S(1)}, u32[]{:S(2)}, u32[]{:S(2)}) collective-permute-start(f32[3,64,128]{1,2,0:T(8,128)S(1)} %get-tuple-element.400), channel_id=1, source_target_pairs={{0,2},{1,3},{2,4},{3,5},{4,6},{5,7},{6,8},{7,9},{8,10},{9,11},{10,... | collective-permute-start | bytes 294920 | tf_op jit(solution)/shard_map/ppermute | solution.py:16
  140.1 2.1 collective-permute-start.18
  142.8 1.5 collective-permute-start.23
  144.9 5.7 %collective-permute-done.23 = f32[3,64,64]{1,2,0:T(8,128)S(1)} collective-permute-done((f32[3,64,64]{1,2,0:T(8,128)S(1)}, f32[3,64,64]{1,2,0:T(8,128)S(1)}, u32[]{:S(2)}, u32[]{:S(2)}) %collective-permute-start.23) | collective-permute-done | bytes 49184 | tf_op jit(solution)/shard_map/ppermute | solution.py:16
  151.3 0.9 gather_fusion.26
  164.1 1.3 collective-permute-start.28
  165.4 1.3 collective-permute-start.27
  166.7 1.3 collective-permute-start.29
  168.6 5.5 %collective-permute-start.25 = (f32[3,64,128]{1,2,0:T(8,128)S(1)}, f32[3,64,128]{1,2,0:T(8,128)S(1)}, u32[]{:S(2)}, u32[]{:S(2)}) collective-permute-start(f32[3,64,128]{1,2,0:T(8,128)S(1)} %get-tuple-element.398), channel_id=1, source_target_pairs={{0,2},{1,3},{2,4},{3,5},{4,6},{5,7},{6,8},{7,9},{8,10},{9,11},{10,... | collective-permute-start | bytes 294920 | tf_op jit(solution)/shard_map/ppermute | solution.py:16
  174.2 3.0 %collective-permute-start.24 = (f32[3,64,128]{1,2,0:T(8,128)S(1)}, f32[3,64,128]{1,2,0:T(8,128)S(1)}, u32[]{:S(2)}, u32[]{:S(2)}) collective-permute-start(f32[3,64,128]{1,2,0:T(8,128)S(1)} %get-tuple-element.398), channel_id=1, source_target_pairs={{0,1},{1,2},{2,3},{3,4},{4,5},{5,6},{6,7},{7,8},{8,9},{9,10},{10,1... | collective-permute-start | bytes 294920 | tf_op jit(solution)/shard_map/ppermute | solution.py:16
  177.7 5.5 %collective-permute-start.26 = (f32[3,64,64]{1,2,0:T(8,128)}, f32[3,64,64]{1,2,0:T(8,128)S(1)}, u32[]{:S(2)}, u32[]{:S(2)}) collective-permute-start(f32[3,64,64]{1,2,0:T(8,128)} %constant_dynamic-slice_fusion), channel_id=1, source_target_pairs={{0,3},{1,4},{2,5},{3,6},{4,7},{5,8},{6,9},{7,10},{8,11},{9,12},{10... | collective-permute-start | bytes 147464 | tf_op jit(solution)/shard_map/ppermute | solution.py:16
  183.8 1.9 collective-permute-done.26
  186.4 0.9 gather_fusion.32
  197.4 0.8 multiply_reduce_fusion.1
  198.2 43.2 %all-reduce.5 = (f32[]{:T(128)}, f32[]{:T(128)}, f32[]{:T(128)}, f32[]{:T(128)}, f32[]{:T(128)}) all-reduce(f32[]{:T(128)} %get-tuple-element.375, f32[]{:T(128)} %get-tuple-element.376, f32[]{:T(128)} %get-tuple-element.377, f32[]{:T(128)} %get-tuple-element.374, ...), channel_id=1, replica_groups=mesh['curve'=8,'level'=4] {'curve','level'}, use_global_device_ids=true, to_apply=%region_2.5 | all-reduce | flops 5 | bytes 40 | tf_op jit(solution)/shard_map/psum | solution.py:130
  244.8 0.8 copy.270
  245.6 0.8 copy.271
  (460 shorter events, 65.9 us)
Async XLA Ops:
  2.5 1.1 copy-start.55
  4.5 44.2 %collective-permute-start.4 = (f32[3,64,128]{1,2,0:T(8,128)S(1)}, f32[3,64,128]{1,2,0:T(8,128)S(1)}, u32[]{:S(2)}, u32[]{:S(2)}) collective-permute-start(f32[3,64,128]{1,2,0:T(8,128)S(1)} %get-tuple-element.403), channel_id=1, source_target_pairs={{2,0},{3,1},{4,2},{5,3},{6,4},{7,5},{8,6},{9,7},{10,8},{11,9},{12,... | collective-permute-start | bytes 294920 | tf_op jit(solution)/shard_map/ppermute | solution.py:16
  5.8 42.9 %collective-permute-start.3 = (f32[3,64,128]{1,2,0:T(8,128)S(1)}, f32[3,64,128]{1,2,0:T(8,128)S(1)}, u32[]{:S(2)}, u32[]{:S(2)}) collective-permute-start(f32[3,64,128]{1,2,0:T(8,128)S(1)} %get-tuple-element.403), channel_id=1, source_target_pairs={{1,0},{2,1},{3,2},{4,3},{5,4},{6,5},{7,6},{8,7},{9,8},{10,9},{11,1... | collective-permute-start | bytes 294920 | tf_op jit(solution)/shard_map/ppermute | solution.py:16
  7.1 45.5 %collective-permute-start.1 = (f32[3,64,128]{1,2,0:T(8,128)S(1)}, f32[3,64,128]{1,2,0:T(8,128)S(1)}, u32[]{:S(2)}, u32[]{:S(2)}) collective-permute-start(f32[3,64,128]{1,2,0:T(8,128)S(1)} %get-tuple-element.404), channel_id=1, source_target_pairs={{0,2},{1,3},{2,4},{3,5},{4,6},{5,7},{6,8},{7,9},{8,10},{9,11},{10,... | collective-permute-start | bytes 294920 | tf_op jit(solution)/shard_map/ppermute | solution.py:16
  13.3 40.3 %collective-permute-start = (f32[3,64,128]{1,2,0:T(8,128)S(1)}, f32[3,64,128]{1,2,0:T(8,128)S(1)}, u32[]{:S(2)}, u32[]{:S(2)}) collective-permute-start(f32[3,64,128]{1,2,0:T(8,128)S(1)} %get-tuple-element.404), channel_id=1, source_target_pairs={{0,1},{1,2},{2,3},{3,4},{4,5},{5,6},{6,7},{7,8},{8,9},{9,10},{10,1... | collective-permute-start | bytes 294920 | tf_op jit(solution)/shard_map/ppermute | solution.py:16
  16.1 26.6 %collective-permute-start.2 = (f32[3,64,64]{1,2,0:T(8,128)S(1)}, f32[3,64,64]{1,2,0:T(8,128)S(1)}, u32[]{:S(2)}, u32[]{:S(2)}) collective-permute-start(f32[3,64,64]{1,2,0:T(8,128)S(1)} %constant_dynamic-slice_fusion.4), channel_id=1, source_target_pairs={{0,3},{1,4},{2,5},{3,6},{4,7},{5,8},{6,9},{7,10},{8,11},{9,12},{10... | collective-permute-start | bytes 147464 | tf_op jit(solution)/shard_map/ppermute | solution.py:16
  28.5 4.8 %copy-start.1 = (s32[3]{0:T(128)S(1)}, s32[3]{0:T(128)}, u32[]{:S(2)}) copy-start(s32[3]{0:T(128)} %constant.873.clone) | copy-start | bytes 40
  38.7 12.5 %copy-start.43 = (pred[128]{0:T(512)(128)(4,1)}, pred[128]{0:T(512)(128)(4,1)S(1)}, u32[]{:S(2)}) copy-start(pred[128]{0:T(512)(128)(4,1)S(1)} %get-tuple-element.541) | copy-start | bytes 388
  38.7 56.1 %copy-start.20 = (pred[128]{0:T(512)(128)(4,1)}, pred[128]{0:T(512)(128)(4,1)S(1)}, u32[]{:S(2)}) copy-start(pred[128]{0:T(512)(128)(4,1)S(1)} %get-tuple-element.543) | copy-start | bytes 388
  42.8 5.9 %collective-permute-start.5 = (f32[3,64,64]{1,2,0:T(8,128)S(1)}, f32[3,64,64]{1,2,0:T(8,128)S(1)}, u32[]{:S(2)}, u32[]{:S(2)}) collective-permute-start(f32[3,64,64]{1,2,0:T(8,128)S(1)} %slice.1835), channel_id=1, source_target_pairs={{3,0},{4,1},{5,2},{6,3},{7,4},{8,5},{9,6},{10,7},{11,8},{12,9},{13... | collective-permute-start | bytes 147464 | tf_op jit(solution)/shard_map/ppermute | solution.py:16
  60.4 15.2 %collective-permute-start.8 = (f32[3,64,64]{1,2,0:T(8,128)S(1)}, f32[3,64,64]{1,2,0:T(8,128)S(1)}, u32[]{:S(2)}, u32[]{:S(2)}) collective-permute-start(f32[3,64,64]{1,2,0:T(8,128)S(1)} %constant_dynamic-slice_fusion.3), channel_id=1, source_target_pairs={{0,3},{1,4},{2,5},{3,6},{4,7},{5,8},{6,9},{7,10},{8,11},{9,12},{10... | collective-permute-start | bytes 147464 | tf_op jit(solution)/shard_map/ppermute | solution.py:16
  63.8 20.9 %collective-permute-start.10 = (f32[3,64,128]{1,2,0:T(8,128)S(1)}, f32[3,64,128]{1,2,0:T(8,128)S(1)}, u32[]{:S(2)}, u32[]{:S(2)}) collective-permute-start(f32[3,64,128]{1,2,0:T(8,128)S(1)} %get-tuple-element.401), channel_id=1, source_target_pairs={{2,0},{3,1},{4,2},{5,3},{6,4},{7,5},{8,6},{9,7},{10,8},{11,9},{12,... | collective-permute-start | bytes 294920 | tf_op jit(solution)/shard_map/ppermute | solution.py:16
  65.1 19.6 %collective-permute-start.9 = (f32[3,64,128]{1,2,0:T(8,128)S(1)}, f32[3,64,128]{1,2,0:T(8,128)S(1)}, u32[]{:S(2)}, u32[]{:S(2)}) collective-permute-start(f32[3,64,128]{1,2,0:T(8,128)S(1)} %get-tuple-element.401), channel_id=1, source_target_pairs={{1,0},{2,1},{3,2},{4,3},{5,4},{6,5},{7,6},{8,7},{9,8},{10,9},{11,1... | collective-permute-start | bytes 294920 | tf_op jit(solution)/shard_map/ppermute | solution.py:16
  66.4 22.4 %collective-permute-start.7 = (f32[3,64,128]{1,2,0:T(8,128)S(1)}, f32[3,64,128]{1,2,0:T(8,128)S(1)}, u32[]{:S(2)}, u32[]{:S(2)}) collective-permute-start(f32[3,64,128]{1,2,0:T(8,128)S(1)} %get-tuple-element.402), channel_id=1, source_target_pairs={{0,2},{1,3},{2,4},{3,5},{4,6},{5,7},{6,8},{7,9},{8,10},{9,11},{10,... | collective-permute-start | bytes 294920 | tf_op jit(solution)/shard_map/ppermute | solution.py:16
  71.8 18.1 %collective-permute-start.6 = (f32[3,64,128]{1,2,0:T(8,128)S(1)}, f32[3,64,128]{1,2,0:T(8,128)S(1)}, u32[]{:S(2)}, u32[]{:S(2)}) collective-permute-start(f32[3,64,128]{1,2,0:T(8,128)S(1)} %get-tuple-element.402), channel_id=1, source_target_pairs={{0,1},{1,2},{2,3},{3,4},{4,5},{5,6},{6,7},{7,8},{8,9},{9,10},{10,1... | collective-permute-start | bytes 294920 | tf_op jit(solution)/shard_map/ppermute | solution.py:16
  75.6 8.4 %collective-permute-start.11 = (f32[3,64,64]{1,2,0:T(8,128)S(1)}, f32[3,64,64]{1,2,0:T(8,128)S(1)}, u32[]{:S(2)}, u32[]{:S(2)}) collective-permute-start(f32[3,64,64]{1,2,0:T(8,128)S(1)} %slice.1866), channel_id=1, source_target_pairs={{3,0},{4,1},{5,2},{6,3},{7,4},{8,5},{9,6},{10,7},{11,8},{12,9},{13... | collective-permute-start | bytes 147464 | tf_op jit(solution)/shard_map/ppermute | solution.py:16
  84.8 0.9 copy-start.40
  84.8 0.9 copy-start.52
  86.5 0.8 copy-start.36
  86.5 0.8 copy-start.48
  97.2 14.7 %collective-permute-start.14 = (f32[3,16,64]{2,1,0:T(8,128)S(1)}, f32[3,16,64]{2,1,0:T(8,128)S(1)}, u32[]{:S(2)}, u32[]{:S(2)}) collective-permute-start(f32[3,16,64]{2,1,0:T(8,128)S(1)} %constant_dynamic-slice_fusion.2), channel_id=1, source_target_pairs={{0,3},{1,4},{2,5},{3,6},{4,7},{5,8},{6,9},{7,10},{8,11},{9,12},{10... | collective-permute-start | bytes 36872 | tf_op jit(solution)/shard_map/ppermute | solution.py:16
  101.1 20.9 %collective-permute-start.16 = (f32[3,16,128]{2,1,0:T(8,128)S(1)}, f32[3,16,128]{2,1,0:T(8,128)S(1)}, u32[]{:S(2)}, u32[]{:S(2)}) collective-permute-start(f32[3,16,128]{2,1,0:T(8,128)S(1)} %get-tuple-element.509), channel_id=1, source_target_pairs={{2,0},{3,1},{4,2},{5,3},{6,4},{7,5},{8,6},{9,7},{10,8},{11,9},{12,... | collective-permute-start | bytes 73736 | tf_op jit(solution)/shard_map/ppermute | solution.py:16
  102.4 19.8 %collective-permute-start.15 = (f32[3,16,128]{2,1,0:T(8,128)S(1)}, f32[3,16,128]{2,1,0:T(8,128)S(1)}, u32[]{:S(2)}, u32[]{:S(2)}) collective-permute-start(f32[3,16,128]{2,1,0:T(8,128)S(1)} %get-tuple-element.509), channel_id=1, source_target_pairs={{1,0},{2,1},{3,2},{4,3},{5,4},{6,5},{7,6},{8,7},{9,8},{10,9},{11,1... | collective-permute-start | bytes 73736 | tf_op jit(solution)/shard_map/ppermute | solution.py:16
  103.7 15.2 %collective-permute-start.13 = (f32[3,16,128]{2,1,0:T(8,128)S(1)}, f32[3,16,128]{2,1,0:T(8,128)S(1)}, u32[]{:S(2)}, u32[]{:S(2)}) collective-permute-start(f32[3,16,128]{2,1,0:T(8,128)S(1)} %get-tuple-element.510), channel_id=1, source_target_pairs={{0,2},{1,3},{2,4},{3,5},{4,6},{5,7},{6,8},{7,9},{8,10},{9,11},{10,... | collective-permute-start | bytes 73736 | tf_op jit(solution)/shard_map/ppermute | solution.py:16
  109.7 9.2 %collective-permute-start.12 = (f32[3,16,128]{2,1,0:T(8,128)S(1)}, f32[3,16,128]{2,1,0:T(8,128)S(1)}, u32[]{:S(2)}, u32[]{:S(2)}) collective-permute-start(f32[3,16,128]{2,1,0:T(8,128)S(1)} %get-tuple-element.510), channel_id=1, source_target_pairs={{0,1},{1,2},{2,3},{3,4},{4,5},{5,6},{6,7},{7,8},{8,9},{9,10},{10,1... | collective-permute-start | bytes 73736 | tf_op jit(solution)/shard_map/ppermute | solution.py:16
  111.9 7.0 %collective-permute-start.17 = (f32[3,16,64]{2,1,0:T(8,128)S(1)}, f32[3,16,64]{2,1,0:T(8,128)S(1)}, u32[]{:S(2)}, u32[]{:S(2)}) collective-permute-start(f32[3,16,64]{2,1,0:T(8,128)S(1)} %bitcast.526), channel_id=1, source_target_pairs={{3,0},{4,1},{5,2},{6,3},{7,4},{8,5},{9,6},{10,7},{11,8},{12,9},{13... | collective-permute-start | bytes 36872 | tf_op jit(solution)/shard_map/ppermute | solution.py:16
  127.3 15.5 %collective-permute-start.20 = (f32[3,64,64]{1,2,0:T(8,128)S(1)}, f32[3,64,64]{1,2,0:T(8,128)S(1)}, u32[]{:S(2)}, u32[]{:S(2)}) collective-permute-start(f32[3,64,64]{1,2,0:T(8,128)S(1)} %constant_dynamic-slice_fusion.1), channel_id=1, source_target_pairs={{0,3},{1,4},{2,5},{3,6},{4,7},{5,8},{6,9},{7,10},{8,11},{9,12},{10... | collective-permute-start | bytes 147464 | tf_op jit(solution)/shard_map/ppermute | solution.py:16
  131.3 19.8 %collective-permute-start.22 = (f32[3,64,128]{1,2,0:T(8,128)S(1)}, f32[3,64,128]{1,2,0:T(8,128)S(1)}, u32[]{:S(2)}, u32[]{:S(2)}) collective-permute-start(f32[3,64,128]{1,2,0:T(8,128)S(1)} %get-tuple-element.399), channel_id=1, source_target_pairs={{2,0},{3,1},{4,2},{5,3},{6,4},{7,5},{8,6},{9,7},{10,8},{11,9},{12,... | collective-permute-start | bytes 294920 | tf_op jit(solution)/shard_map/ppermute | solution.py:16
  132.6 18.6 %collective-permute-start.21 = (f32[3,64,128]{1,2,0:T(8,128)S(1)}, f32[3,64,128]{1,2,0:T(8,128)S(1)}, u32[]{:S(2)}, u32[]{:S(2)}) collective-permute-start(f32[3,64,128]{1,2,0:T(8,128)S(1)} %get-tuple-element.399), channel_id=1, source_target_pairs={{1,0},{2,1},{3,2},{4,3},{5,4},{6,5},{7,6},{8,7},{9,8},{10,9},{11,1... | collective-permute-start | bytes 294920 | tf_op jit(solution)/shard_map/ppermute | solution.py:16
  133.9 21.4 %collective-permute-start.19 = (f32[3,64,128]{1,2,0:T(8,128)S(1)}, f32[3,64,128]{1,2,0:T(8,128)S(1)}, u32[]{:S(2)}, u32[]{:S(2)}) collective-permute-start(f32[3,64,128]{1,2,0:T(8,128)S(1)} %get-tuple-element.400), channel_id=1, source_target_pairs={{0,2},{1,3},{2,4},{3,5},{4,6},{5,7},{6,8},{7,9},{8,10},{9,11},{10,... | collective-permute-start | bytes 294920 | tf_op jit(solution)/shard_map/ppermute | solution.py:16
  140.1 16.2 %collective-permute-start.18 = (f32[3,64,128]{1,2,0:T(8,128)S(1)}, f32[3,64,128]{1,2,0:T(8,128)S(1)}, u32[]{:S(2)}, u32[]{:S(2)}) collective-permute-start(f32[3,64,128]{1,2,0:T(8,128)S(1)} %get-tuple-element.400), channel_id=1, source_target_pairs={{0,1},{1,2},{2,3},{3,4},{4,5},{5,6},{6,7},{7,8},{8,9},{9,10},{10,1... | collective-permute-start | bytes 294920 | tf_op jit(solution)/shard_map/ppermute | solution.py:16
  142.8 7.8 %collective-permute-start.23 = (f32[3,64,64]{1,2,0:T(8,128)S(1)}, f32[3,64,64]{1,2,0:T(8,128)S(1)}, u32[]{:S(2)}, u32[]{:S(2)}) collective-permute-start(f32[3,64,64]{1,2,0:T(8,128)S(1)} %slice.1928), channel_id=1, source_target_pairs={{3,0},{4,1},{5,2},{6,3},{7,4},{8,5},{9,6},{10,7},{11,8},{12,9},{13... | collective-permute-start | bytes 147464 | tf_op jit(solution)/shard_map/ppermute | solution.py:16
  151.3 0.9 copy-start.41
  151.3 0.9 copy-start.53
  153.0 0.8 copy-start.37
  153.0 0.8 copy-start.49
  157.1 0.8 copy-start.19
  157.2 0.8 copy-start.33
  164.1 22.2 %collective-permute-start.28 = (f32[3,64,128]{1,2,0:T(8,128)S(1)}, f32[3,64,128]{1,2,0:T(8,128)S(1)}, u32[]{:S(2)}, u32[]{:S(2)}) collective-permute-start(f32[3,64,128]{1,2,0:T(8,128)S(1)} %get-tuple-element.397), channel_id=1, source_target_pairs={{2,0},{3,1},{4,2},{5,3},{6,4},{7,5},{8,6},{9,7},{10,8},{11,9},{12,... | collective-permute-start | bytes 294920 | tf_op jit(solution)/shard_map/ppermute | solution.py:16
  165.4 20.9 %collective-permute-start.27 = (f32[3,64,128]{1,2,0:T(8,128)S(1)}, f32[3,64,128]{1,2,0:T(8,128)S(1)}, u32[]{:S(2)}, u32[]{:S(2)}) collective-permute-start(f32[3,64,128]{1,2,0:T(8,128)S(1)} %get-tuple-element.397), channel_id=1, source_target_pairs={{1,0},{2,1},{3,2},{4,3},{5,4},{6,5},{7,6},{8,7},{9,8},{10,9},{11,1... | collective-permute-start | bytes 294920 | tf_op jit(solution)/shard_map/ppermute | solution.py:16
  166.7 11.0 %collective-permute-start.29 = (f32[3,64,64]{1,2,0:T(8,128)S(1)}, f32[3,64,64]{1,2,0:T(8,128)S(1)}, u32[]{:S(2)}, u32[]{:S(2)}) collective-permute-start(f32[3,64,64]{1,2,0:T(8,128)S(1)} %slice.1959), channel_id=1, source_target_pairs={{3,0},{4,1},{5,2},{6,3},{7,4},{8,5},{9,6},{10,7},{11,8},{12,9},{13... | collective-permute-start | bytes 147464 | tf_op jit(solution)/shard_map/ppermute | solution.py:16
  168.6 21.8 %collective-permute-start.25 = (f32[3,64,128]{1,2,0:T(8,128)S(1)}, f32[3,64,128]{1,2,0:T(8,128)S(1)}, u32[]{:S(2)}, u32[]{:S(2)}) collective-permute-start(f32[3,64,128]{1,2,0:T(8,128)S(1)} %get-tuple-element.398), channel_id=1, source_target_pairs={{0,2},{1,3},{2,4},{3,5},{4,6},{5,7},{6,8},{7,9},{8,10},{9,11},{10,... | collective-permute-start | bytes 294920 | tf_op jit(solution)/shard_map/ppermute | solution.py:16
  174.2 17.3 %collective-permute-start.24 = (f32[3,64,128]{1,2,0:T(8,128)S(1)}, f32[3,64,128]{1,2,0:T(8,128)S(1)}, u32[]{:S(2)}, u32[]{:S(2)}) collective-permute-start(f32[3,64,128]{1,2,0:T(8,128)S(1)} %get-tuple-element.398), channel_id=1, source_target_pairs={{0,1},{1,2},{2,3},{3,4},{4,5},{5,6},{6,7},{7,8},{8,9},{9,10},{10,1... | collective-permute-start | bytes 294920 | tf_op jit(solution)/shard_map/ppermute | solution.py:16
  177.7 8.0 %collective-permute-start.26 = (f32[3,64,64]{1,2,0:T(8,128)}, f32[3,64,64]{1,2,0:T(8,128)S(1)}, u32[]{:S(2)}, u32[]{:S(2)}) collective-permute-start(f32[3,64,64]{1,2,0:T(8,128)} %constant_dynamic-slice_fusion), channel_id=1, source_target_pairs={{0,3},{1,4},{2,5},{3,6},{4,7},{5,8},{6,9},{7,10},{8,11},{9,12},{10... | collective-permute-start | bytes 147464 | tf_op jit(solution)/shard_map/ppermute | solution.py:16
  186.4 0.9 copy-start.42
  186.4 0.9 copy-start.54
  188.1 0.8 copy-start.38
  188.1 0.8 copy-start.50
  (42 other events, 29.3 us)
where the time goes:
time: 250 us; the launch traced here: 248 us
  starting transfers between devices  83.7 us (33%)
  local copies, waits for them, and re-layouts  76.8 us (31%)
  blocking collectives  43.2 us (17%)
  waiting for transfers between devices  24.4 us (10%)
  other arithmetic  11.1 us (4%)
  between operations  8.26 us (3%)
    ppermute x30, starting transfers between devices, from_behind(): return lax.ppermute(block, axis, route)  83.7 us
    psum x1, blocking collectives, local(): lax.psum((local_along, local_curvature, jnp.sum(residual_in * residual_in...  43.2 us
    ppermute x30, waiting for transfers between devices, from_behind(): return lax.ppermute(block, axis, route)  24.4 us
    gather x30, local copies, waits for them, and re-layouts, exchange(): picked = jnp.take(lookup, position[face_id], axis=1)  23.5 us
    unnamed x148, local copies, waits for them, and re-layouts  20.8 us
  transfers between devices with their start and end apart: 30, of which 5 were waited for; matrix products, arithmetic and copies ran while one was open for 17% of the time, Pallas kernels for 0%

commit v1 on v0

--- a/solution.py
+++ b/solution.py
@@ -128,14 +128,17 @@
     local_along = jnp.sum(residual_in * preconditioned)
     local_curvature = jnp.sum(preconditioned * image)
     along, curvature, old_square, cross_term, image_square = lax.psum(
-        (
-            local_along,
-            local_curvature,
-            jnp.sum(residual_in * residual_in),
-            jnp.sum(residual_in * image),
-            jnp.sum(image * image),
+        lax.psum(
+            (
+                local_along,
+                local_curvature,
+                jnp.sum(residual_in * residual_in),
+                jnp.sum(residual_in * image),
+                jnp.sum(image * image),
+            ),
+            "curve",
         ),
-        ("curve", "level"),
+        "level",
     )
     step_size = along / curvature
     solution = step_size * preconditioned

time: 250 us -> 236 us (0.944)
  blocking collectives: 43.2 us -> 29.1 us
    psum x1, blocking collectives: 43.2 us -> 22.4 us  [local(): lax.psum((local_along, local_curvature, jnp.sum(residual_in * residual_in...]
    psum x0 -> x1, blocking collectives: none -> 6.73 us  [local(): lax.psum(lax.psum((local_along, local_curvature, jnp.sum(residual_in * re...]
  transfers between devices with their start and end apart: 30 -> 30, of which waited for: 5 -> 5; matrix products, arithmetic and copies ran while one was open for 17% -> 18% of each run, Pallas kernels for 0% -> 0%
where the time goes in v1:
time: 236 us; the launch traced here: 234 us
  starting transfers between devices  83.7 us (35%)
  local copies, waits for them, and re-layouts  77.1 us (33%)
  blocking collectives  29.1 us (12%)
  waiting for transfers between devices  24.5 us (10%)
  other arithmetic  11.2 us (5%)
  between operations  8.32 us (4%)
    ppermute x30, starting transfers between devices, from_behind(): return lax.ppermute(block, axis, route)  83.7 us
    ppermute x30, waiting for transfers between devices, from_behind(): return lax.ppermute(block, axis, route)  24.5 us
    gather x30, local copies, waits for them, and re-layouts, exchange(): picked = jnp.take(lookup, position[face_id], axis=1)  23.5 us
    psum x1, blocking collectives, local(): lax.psum((local_along, local_curvature, jnp.sum(residual_in * residual_in...  22.4 us
    unnamed x148, local copies, waits for them, and re-layouts  21.1 us
    psum x1, blocking collectives, local(): lax.psum(lax.psum((local_along, local_curvature, jnp.sum(residual_in * re...  6.73 us
    gather x1, local copies, waits for them, and re-layouts, local(): counts[owner] - width_table[hop_index]  4.79 us
    gather x1, local copies, waits for them, and re-layouts, local(): start_table[hop_index] + offset - skipped  4.79 us
  transfers between devices with their start and end apart: 30, of which 5 were waited for; matrix products, arithmetic and copies ran while one was open for 18% of the time, Pallas kernels for 0%

profile of v1, /device:TPU:0, one launch (start us, length us, event | category | flops | bytes accessed | tf_op | source)
XLA Modules:
  0.0 233.8 jit_solution(12254014277037834243)
XLA Ops:
  2.5 1.1 copy.169
  4.5 1.3 collective-permute-start.4
  5.8 1.3 collective-permute-start.3
  7.1 6.2 %collective-permute-start.1 = (f32[3,64,128]{1,2,0:T(8,128)S(1)}, f32[3,64,128]{1,2,0:T(8,128)S(1)}, u32[]{:S(2)}, u32[]{:S(2)}) collective-permute-start(f32[3,64,128]{1,2,0:T(8,128)S(1)} %get-tuple-element.409), channel_id=1, source_target_pairs={{0,2},{1,3},{2,4},{3,5},{4,6},{5,7},{6,8},{7,9},{8,10},{9,11},{10,... | collective-permute-start | bytes 294920 | tf_op jit(solution)/shard_map/ppermute | solution.py:16
  13.3 2.1 collective-permute-start
  16.1 5.5 %collective-permute-start.2 = (f32[3,64,64]{1,2,0:T(8,128)S(1)}, f32[3,64,64]{1,2,0:T(8,128)S(1)}, u32[]{:S(2)}, u32[]{:S(2)}) collective-permute-start(f32[3,64,64]{1,2,0:T(8,128)S(1)} %constant_dynamic-slice_fusion.4), channel_id=1, source_target_pairs={{0,3},{1,4},{2,5},{3,6},{4,7},{5,8},{6,9},{7,10},{8,11},{9,12},{10... | collective-permute-start | bytes 147464 | tf_op jit(solution)/shard_map/ppermute | solution.py:16
  23.0 4.8 %gather_fusion.1 = s32[768]{0:T(1024)S(1)} fusion(s32[32]{0:T(128)S(1)} %copy-done, s32[1024]{0:T(1024)S(1)} %get-tuple-element.560), kind=kCustom, calls=%fused_computation.31 | custom fusion | bytes 9216 | tf_op jit(solution)/shard_map/gather | solution.py:102
  28.5 4.8 %gather_fusion.2 = s32[768]{0:T(1024)S(1)} fusion(s32[3]{0:T(128)S(1)} %copy-done.2, s32[1024]{0:T(1024)S(1)} %get-tuple-element.561), kind=kCustom, calls=%fused_computation.32 | custom fusion | bytes 9216 | tf_op jit(solution)/shard_map/gather | solution.py:102
  33.3 4.8 %gather_fusion = s32[768]{0:T(1024)S(1)} fusion(s32[3]{0:T(128)S(1)} %copy-done.1, s32[1024]{0:T(1024)S(1)} %get-tuple-element.561), kind=kCustom, calls=%fused_computation.30 | custom fusion | bytes 9216 | tf_op jit(solution)/shard_map/gather | solution.py:103
  42.8 1.3 collective-permute-start.5
  44.1 4.6 %collective-permute-done.5 = f32[3,64,64]{1,2,0:T(8,128)S(1)} collective-permute-done((f32[3,64,64]{1,2,0:T(8,128)S(1)}, f32[3,64,64]{1,2,0:T(8,128)S(1)}, u32[]{:S(2)}, u32[]{:S(2)}) %collective-permute-start.5) | collective-permute-done | bytes 49184 | tf_op jit(solution)/shard_map/ppermute | solution.py:16
  56.3 0.8 gather_fusion.5
  60.6 3.3 %collective-permute-start.8 = (f32[3,64,64]{1,2,0:T(8,128)S(1)}, f32[3,64,64]{1,2,0:T(8,128)S(1)}, u32[]{:S(2)}, u32[]{:S(2)}) collective-permute-start(f32[3,64,64]{1,2,0:T(8,128)S(1)} %constant_dynamic-slice_fusion.3), channel_id=1, source_target_pairs={{0,3},{1,4},{2,5},{3,6},{4,7},{5,8},{6,9},{7,10},{8,11},{9,12},{10... | collective-permute-start | bytes 147464 | tf_op jit(solution)/shard_map/ppermute | solution.py:16
  64.0 1.3 collective-permute-start.10
  65.3 1.3 collective-permute-start.9
  66.6 5.4 %collective-permute-start.7 = (f32[3,64,128]{1,2,0:T(8,128)S(1)}, f32[3,64,128]{1,2,0:T(8,128)S(1)}, u32[]{:S(2)}, u32[]{:S(2)}) collective-permute-start(f32[3,64,128]{1,2,0:T(8,128)S(1)} %get-tuple-element.407), channel_id=1, source_target_pairs={{0,2},{1,3},{2,4},{3,5},{4,6},{5,7},{6,8},{7,9},{8,10},{9,11},{10,... | collective-permute-start | bytes 294920 | tf_op jit(solution)/shard_map/ppermute | solution.py:16
  72.1 3.3 %collective-permute-start.6 = (f32[3,64,128]{1,2,0:T(8,128)S(1)}, f32[3,64,128]{1,2,0:T(8,128)S(1)}, u32[]{:S(2)}, u32[]{:S(2)}) collective-permute-start(f32[3,64,128]{1,2,0:T(8,128)S(1)} %get-tuple-element.407), channel_id=1, source_target_pairs={{0,1},{1,2},{2,3},{3,4},{4,5},{5,6},{6,7},{7,8},{8,9},{9,10},{10,1... | collective-permute-start | bytes 294920 | tf_op jit(solution)/shard_map/ppermute | solution.py:16
  75.8 1.3 collective-permute-start.11
  77.8 6.5 %collective-permute-done.11 = f32[3,64,64]{1,2,0:T(8,128)S(1)} collective-permute-done((f32[3,64,64]{1,2,0:T(8,128)S(1)}, f32[3,64,64]{1,2,0:T(8,128)S(1)}, u32[]{:S(2)}, u32[]{:S(2)}) %collective-permute-start.11) | collective-permute-done | bytes 49184 | tf_op jit(solution)/shard_map/ppermute | solution.py:16
  85.0 0.9 gather_fusion.14
  97.4 3.9 %collective-permute-start.14 = (f32[3,16,64]{2,1,0:T(8,128)S(1)}, f32[3,16,64]{2,1,0:T(8,128)S(1)}, u32[]{:S(2)}, u32[]{:S(2)}) collective-permute-start(f32[3,16,64]{2,1,0:T(8,128)S(1)} %constant_dynamic-slice_fusion.2), channel_id=1, source_target_pairs={{0,3},{1,4},{2,5},{3,6},{4,7},{5,8},{6,9},{7,10},{8,11},{9,12},{10... | collective-permute-start | bytes 36872 | tf_op jit(solution)/shard_map/ppermute | solution.py:16
  101.4 1.3 collective-permute-start.16
  102.7 1.3 collective-permute-start.15
  104.0 6.0 %collective-permute-start.13 = (f32[3,16,128]{2,1,0:T(8,128)S(1)}, f32[3,16,128]{2,1,0:T(8,128)S(1)}, u32[]{:S(2)}, u32[]{:S(2)}) collective-permute-start(f32[3,16,128]{2,1,0:T(8,128)S(1)} %get-tuple-element.515), channel_id=1, source_target_pairs={{0,2},{1,3},{2,4},{3,5},{4,6},{5,7},{6,8},{7,9},{8,10},{9,11},{10,... | collective-permute-start | bytes 73736 | tf_op jit(solution)/shard_map/ppermute | solution.py:16
  110.0 2.1 collective-permute-start.12
  112.1 1.3 collective-permute-start.17
  113.4 5.7 %collective-permute-done.17 = f32[3,16,64]{2,1,0:T(8,128)S(1)} collective-permute-done((f32[3,16,64]{2,1,0:T(8,128)S(1)}, f32[3,16,64]{2,1,0:T(8,128)S(1)}, u32[]{:S(2)}, u32[]{:S(2)}) %collective-permute-start.17) | collective-permute-done | bytes 12320 | tf_op jit(solution)/shard_map/ppermute | solution.py:16
  127.5 3.9 %collective-permute-start.20 = (f32[3,64,64]{1,2,0:T(8,128)S(1)}, f32[3,64,64]{1,2,0:T(8,128)S(1)}, u32[]{:S(2)}, u32[]{:S(2)}) collective-permute-start(f32[3,64,64]{1,2,0:T(8,128)S(1)} %constant_dynamic-slice_fusion.1), channel_id=1, source_target_pairs={{0,3},{1,4},{2,5},{3,6},{4,7},{5,8},{6,9},{7,10},{8,11},{9,12},{10... | collective-permute-start | bytes 147464 | tf_op jit(solution)/shard_map/ppermute | solution.py:16
  131.6 1.3 collective-permute-start.22
  132.9 1.3 collective-permute-start.21
  134.2 6.2 %collective-permute-start.19 = (f32[3,64,128]{1,2,0:T(8,128)S(1)}, f32[3,64,128]{1,2,0:T(8,128)S(1)}, u32[]{:S(2)}, u32[]{:S(2)}) collective-permute-start(f32[3,64,128]{1,2,0:T(8,128)S(1)} %get-tuple-element.405), channel_id=1, source_target_pairs={{0,2},{1,3},{2,4},{3,5},{4,6},{5,7},{6,8},{7,9},{8,10},{9,11},{10,... | collective-permute-start | bytes 294920 | tf_op jit(solution)/shard_map/ppermute | solution.py:16
  140.4 2.1 collective-permute-start.18
  143.0 1.5 collective-permute-start.23
  145.1 5.7 %collective-permute-done.23 = f32[3,64,64]{1,2,0:T(8,128)S(1)} collective-permute-done((f32[3,64,64]{1,2,0:T(8,128)S(1)}, f32[3,64,64]{1,2,0:T(8,128)S(1)}, u32[]{:S(2)}, u32[]{:S(2)}) %collective-permute-start.23) | collective-permute-done | bytes 49184 | tf_op jit(solution)/shard_map/ppermute | solution.py:16
  151.5 0.9 gather_fusion.26
  164.4 1.3 collective-permute-start.28
  165.7 1.3 collective-permute-start.27
  167.0 1.3 collective-permute-start.29
  168.9 5.5 %collective-permute-start.25 = (f32[3,64,128]{1,2,0:T(8,128)S(1)}, f32[3,64,128]{1,2,0:T(8,128)S(1)}, u32[]{:S(2)}, u32[]{:S(2)}) collective-permute-start(f32[3,64,128]{1,2,0:T(8,128)S(1)} %get-tuple-element.403), channel_id=1, source_target_pairs={{0,2},{1,3},{2,4},{3,5},{4,6},{5,7},{6,8},{7,9},{8,10},{9,11},{10,... | collective-permute-start | bytes 294920 | tf_op jit(solution)/shard_map/ppermute | solution.py:16
  174.5 3.0 %collective-permute-start.24 = (f32[3,64,128]{1,2,0:T(8,128)S(1)}, f32[3,64,128]{1,2,0:T(8,128)S(1)}, u32[]{:S(2)}, u32[]{:S(2)}) collective-permute-start(f32[3,64,128]{1,2,0:T(8,128)S(1)} %get-tuple-element.403), channel_id=1, source_target_pairs={{0,1},{1,2},{2,3},{3,4},{4,5},{5,6},{6,7},{7,8},{8,9},{9,10},{10,1... | collective-permute-start | bytes 294920 | tf_op jit(solution)/shard_map/ppermute | solution.py:16
  177.9 5.5 %collective-permute-start.26 = (f32[3,64,64]{1,2,0:T(8,128)}, f32[3,64,64]{1,2,0:T(8,128)S(1)}, u32[]{:S(2)}, u32[]{:S(2)}) collective-permute-start(f32[3,64,64]{1,2,0:T(8,128)} %constant_dynamic-slice_fusion), channel_id=1, source_target_pairs={{0,3},{1,4},{2,5},{3,6},{4,7},{5,8},{6,9},{7,10},{8,11},{9,12},{10... | collective-permute-start | bytes 147464 | tf_op jit(solution)/shard_map/ppermute | solution.py:16
  184.0 1.9 collective-permute-done.26
  186.7 0.9 gather_fusion.32
  197.7 0.8 multiply_reduce_fusion.1
  198.5 22.4 %all-reduce.5 = (f32[]{:T(128)}, f32[]{:T(128)}, f32[]{:T(128)}, f32[]{:T(128)}, f32[]{:T(128)}) all-reduce(f32[]{:T(128)} %get-tuple-element.375, f32[]{:T(128)} %get-tuple-element.376, f32[]{:T(128)} %get-tuple-element.377, f32[]{:T(128)} %get-tuple-element.374, f32[]{:T(128)} %get-tuple-element.388), channel_id=1, replica_groups=mesh['curve'=8,'level'=4] {'curve'}, use_global_device_ids=true, to_apply=%region_2.5 | all-reduce | flops 5 | bytes 40 | tf_op jit(solution)/shard_map/psum | solution.py:131
  220.9 6.7 %all-reduce.6 = (f32[]{:T(128)}, f32[]{:T(128)}, f32[]{:T(128)}, f32[]{:T(128)}, f32[]{:T(128)}) all-reduce(f32[]{:T(128)} %get-tuple-element.378, f32[]{:T(128)} %get-tuple-element.379, f32[]{:T(128)} %get-tuple-element.380, f32[]{:T(128)} %get-tuple-element.381, f32[]{:T(128)} %get-tuple-element.382), channel_id=1, replica_groups=mesh['curve'=8,'level'=4] {'level'}, use_global_device_ids=true, to_apply=%region_3.6 | all-reduce | flops 5 | bytes 40 | tf_op jit(solution)/shard_map/psum | solution.py:130
  231.0 0.8 copy.270
  231.9 0.8 copy.271
  (461 shorter events, 66.9 us)
Async XLA Ops:
  2.5 1.1 copy-start.55
  4.5 44.2 %collective-permute-start.4 = (f32[3,64,128]{1,2,0:T(8,128)S(1)}, f32[3,64,128]{1,2,0:T(8,128)S(1)}, u32[]{:S(2)}, u32[]{:S(2)}) collective-permute-start(f32[3,64,128]{1,2,0:T(8,128)S(1)} %get-tuple-element.408), channel_id=1, source_target_pairs={{2,0},{3,1},{4,2},{5,3},{6,4},{7,5},{8,6},{9,7},{10,8},{11,9},{12,... | collective-permute-start | bytes 294920 | tf_op jit(solution)/shard_map/ppermute | solution.py:16
  5.8 43.0 %collective-permute-start.3 = (f32[3,64,128]{1,2,0:T(8,128)S(1)}, f32[3,64,128]{1,2,0:T(8,128)S(1)}, u32[]{:S(2)}, u32[]{:S(2)}) collective-permute-start(f32[3,64,128]{1,2,0:T(8,128)S(1)} %get-tuple-element.408), channel_id=1, source_target_pairs={{1,0},{2,1},{3,2},{4,3},{5,4},{6,5},{7,6},{8,7},{9,8},{10,9},{11,1... | collective-permute-start | bytes 294920 | tf_op jit(solution)/shard_map/ppermute | solution.py:16
  7.1 45.6 %collective-permute-start.1 = (f32[3,64,128]{1,2,0:T(8,128)S(1)}, f32[3,64,128]{1,2,0:T(8,128)S(1)}, u32[]{:S(2)}, u32[]{:S(2)}) collective-permute-start(f32[3,64,128]{1,2,0:T(8,128)S(1)} %get-tuple-element.409), channel_id=1, source_target_pairs={{0,2},{1,3},{2,4},{3,5},{4,6},{5,7},{6,8},{7,9},{8,10},{9,11},{10,... | collective-permute-start | bytes 294920 | tf_op jit(solution)/shard_map/ppermute | solution.py:16
  13.3 40.4 %collective-permute-start = (f32[3,64,128]{1,2,0:T(8,128)S(1)}, f32[3,64,128]{1,2,0:T(8,128)S(1)}, u32[]{:S(2)}, u32[]{:S(2)}) collective-permute-start(f32[3,64,128]{1,2,0:T(8,128)S(1)} %get-tuple-element.409), channel_id=1, source_target_pairs={{0,1},{1,2},{2,3},{3,4},{4,5},{5,6},{6,7},{7,8},{8,9},{9,10},{10,1... | collective-permute-start | bytes 294920 | tf_op jit(solution)/shard_map/ppermute | solution.py:16
  16.1 26.7 %collective-permute-start.2 = (f32[3,64,64]{1,2,0:T(8,128)S(1)}, f32[3,64,64]{1,2,0:T(8,128)S(1)}, u32[]{:S(2)}, u32[]{:S(2)}) collective-permute-start(f32[3,64,64]{1,2,0:T(8,128)S(1)} %constant_dynamic-slice_fusion.4), channel_id=1, source_target_pairs={{0,3},{1,4},{2,5},{3,6},{4,7},{5,8},{6,9},{7,10},{8,11},{9,12},{10... | collective-permute-start | bytes 147464 | tf_op jit(solution)/shard_map/ppermute | solution.py:16
  28.5 4.8 %copy-start.1 = (s32[3]{0:T(128)S(1)}, s32[3]{0:T(128)}, u32[]{:S(2)}) copy-start(s32[3]{0:T(128)} %constant.873.clone) | copy-start | bytes 40
  38.7 12.5 %copy-start.43 = (pred[128]{0:T(512)(128)(4,1)}, pred[128]{0:T(512)(128)(4,1)S(1)}, u32[]{:S(2)}) copy-start(pred[128]{0:T(512)(128)(4,1)S(1)} %get-tuple-element.546) | copy-start | bytes 388
  38.8 56.2 %copy-start.20 = (pred[128]{0:T(512)(128)(4,1)}, pred[128]{0:T(512)(128)(4,1)S(1)}, u32[]{:S(2)}) copy-start(pred[128]{0:T(512)(128)(4,1)S(1)} %get-tuple-element.548) | copy-start | bytes 388
  42.8 5.9 %collective-permute-start.5 = (f32[3,64,64]{1,2,0:T(8,128)S(1)}, f32[3,64,64]{1,2,0:T(8,128)S(1)}, u32[]{:S(2)}, u32[]{:S(2)}) collective-permute-start(f32[3,64,64]{1,2,0:T(8,128)S(1)} %slice.1835), channel_id=1, source_target_pairs={{3,0},{4,1},{5,2},{6,3},{7,4},{8,5},{9,6},{10,7},{11,8},{12,9},{13... | collective-permute-start | bytes 147464 | tf_op jit(solution)/shard_map/ppermute | solution.py:16
  60.6 15.2 %collective-permute-start.8 = (f32[3,64,64]{1,2,0:T(8,128)S(1)}, f32[3,64,64]{1,2,0:T(8,128)S(1)}, u32[]{:S(2)}, u32[]{:S(2)}) collective-permute-start(f32[3,64,64]{1,2,0:T(8,128)S(1)} %constant_dynamic-slice_fusion.3), channel_id=1, source_target_pairs={{0,3},{1,4},{2,5},{3,6},{4,7},{5,8},{6,9},{7,10},{8,11},{9,12},{10... | collective-permute-start | bytes 147464 | tf_op jit(solution)/shard_map/ppermute | solution.py:16
  64.0 20.9 %collective-permute-start.10 = (f32[3,64,128]{1,2,0:T(8,128)S(1)}, f32[3,64,128]{1,2,0:T(8,128)S(1)}, u32[]{:S(2)}, u32[]{:S(2)}) collective-permute-start(f32[3,64,128]{1,2,0:T(8,128)S(1)} %get-tuple-element.406), channel_id=1, source_target_pairs={{2,0},{3,1},{4,2},{5,3},{6,4},{7,5},{8,6},{9,7},{10,8},{11,9},{12,... | collective-permute-start | bytes 294920 | tf_op jit(solution)/shard_map/ppermute | solution.py:16
  65.3 19.6 %collective-permute-start.9 = (f32[3,64,128]{1,2,0:T(8,128)S(1)}, f32[3,64,128]{1,2,0:T(8,128)S(1)}, u32[]{:S(2)}, u32[]{:S(2)}) collective-permute-start(f32[3,64,128]{1,2,0:T(8,128)S(1)} %get-tuple-element.406), channel_id=1, source_target_pairs={{1,0},{2,1},{3,2},{4,3},{5,4},{6,5},{7,6},{8,7},{9,8},{10,9},{11,1... | collective-permute-start | bytes 294920 | tf_op jit(solution)/shard_map/ppermute | solution.py:16
  66.6 22.4 %collective-permute-start.7 = (f32[3,64,128]{1,2,0:T(8,128)S(1)}, f32[3,64,128]{1,2,0:T(8,128)S(1)}, u32[]{:S(2)}, u32[]{:S(2)}) collective-permute-start(f32[3,64,128]{1,2,0:T(8,128)S(1)} %get-tuple-element.407), channel_id=1, source_target_pairs={{0,2},{1,3},{2,4},{3,5},{4,6},{5,7},{6,8},{7,9},{8,10},{9,11},{10,... | collective-permute-start | bytes 294920 | tf_op jit(solution)/shard_map/ppermute | solution.py:16
  72.1 18.0 %collective-permute-start.6 = (f32[3,64,128]{1,2,0:T(8,128)S(1)}, f32[3,64,128]{1,2,0:T(8,128)S(1)}, u32[]{:S(2)}, u32[]{:S(2)}) collective-permute-start(f32[3,64,128]{1,2,0:T(8,128)S(1)} %get-tuple-element.407), channel_id=1, source_target_pairs={{0,1},{1,2},{2,3},{3,4},{4,5},{5,6},{6,7},{7,8},{8,9},{9,10},{10,1... | collective-permute-start | bytes 294920 | tf_op jit(solution)/shard_map/ppermute | solution.py:16
  75.8 8.4 %collective-permute-start.11 = (f32[3,64,64]{1,2,0:T(8,128)S(1)}, f32[3,64,64]{1,2,0:T(8,128)S(1)}, u32[]{:S(2)}, u32[]{:S(2)}) collective-permute-start(f32[3,64,64]{1,2,0:T(8,128)S(1)} %slice.1866), channel_id=1, source_target_pairs={{3,0},{4,1},{5,2},{6,3},{7,4},{8,5},{9,6},{10,7},{11,8},{12,9},{13... | collective-permute-start | bytes 147464 | tf_op jit(solution)/shard_map/ppermute | solution.py:16
  85.0 0.9 copy-start.40
  85.0 0.9 copy-start.52
  86.7 0.8 copy-start.36
  86.7 0.8 copy-start.48
  97.4 14.7 %collective-permute-start.14 = (f32[3,16,64]{2,1,0:T(8,128)S(1)}, f32[3,16,64]{2,1,0:T(8,128)S(1)}, u32[]{:S(2)}, u32[]{:S(2)}) collective-permute-start(f32[3,16,64]{2,1,0:T(8,128)S(1)} %constant_dynamic-slice_fusion.2), channel_id=1, source_target_pairs={{0,3},{1,4},{2,5},{3,6},{4,7},{5,8},{6,9},{7,10},{8,11},{9,12},{10... | collective-permute-start | bytes 36872 | tf_op jit(solution)/shard_map/ppermute | solution.py:16
  101.4 20.9 %collective-permute-start.16 = (f32[3,16,128]{2,1,0:T(8,128)S(1)}, f32[3,16,128]{2,1,0:T(8,128)S(1)}, u32[]{:S(2)}, u32[]{:S(2)}) collective-permute-start(f32[3,16,128]{2,1,0:T(8,128)S(1)} %get-tuple-element.514), channel_id=1, source_target_pairs={{2,0},{3,1},{4,2},{5,3},{6,4},{7,5},{8,6},{9,7},{10,8},{11,9},{12,... | collective-permute-start | bytes 73736 | tf_op jit(solution)/shard_map/ppermute | solution.py:16
  102.7 19.8 %collective-permute-start.15 = (f32[3,16,128]{2,1,0:T(8,128)S(1)}, f32[3,16,128]{2,1,0:T(8,128)S(1)}, u32[]{:S(2)}, u32[]{:S(2)}) collective-permute-start(f32[3,16,128]{2,1,0:T(8,128)S(1)} %get-tuple-element.514), channel_id=1, source_target_pairs={{1,0},{2,1},{3,2},{4,3},{5,4},{6,5},{7,6},{8,7},{9,8},{10,9},{11,1... | collective-permute-start | bytes 73736 | tf_op jit(solution)/shard_map/ppermute | solution.py:16
  104.0 15.2 %collective-permute-start.13 = (f32[3,16,128]{2,1,0:T(8,128)S(1)}, f32[3,16,128]{2,1,0:T(8,128)S(1)}, u32[]{:S(2)}, u32[]{:S(2)}) collective-permute-start(f32[3,16,128]{2,1,0:T(8,128)S(1)} %get-tuple-element.515), channel_id=1, source_target_pairs={{0,2},{1,3},{2,4},{3,5},{4,6},{5,7},{6,8},{7,9},{8,10},{9,11},{10,... | collective-permute-start | bytes 73736 | tf_op jit(solution)/shard_map/ppermute | solution.py:16
  110.0 9.2 %collective-permute-start.12 = (f32[3,16,128]{2,1,0:T(8,128)S(1)}, f32[3,16,128]{2,1,0:T(8,128)S(1)}, u32[]{:S(2)}, u32[]{:S(2)}) collective-permute-start(f32[3,16,128]{2,1,0:T(8,128)S(1)} %get-tuple-element.515), channel_id=1, source_target_pairs={{0,1},{1,2},{2,3},{3,4},{4,5},{5,6},{6,7},{7,8},{8,9},{9,10},{10,1... | collective-permute-start | bytes 73736 | tf_op jit(solution)/shard_map/ppermute | solution.py:16
  112.1 7.0 %collective-permute-start.17 = (f32[3,16,64]{2,1,0:T(8,128)S(1)}, f32[3,16,64]{2,1,0:T(8,128)S(1)}, u32[]{:S(2)}, u32[]{:S(2)}) collective-permute-start(f32[3,16,64]{2,1,0:T(8,128)S(1)} %bitcast.526), channel_id=1, source_target_pairs={{3,0},{4,1},{5,2},{6,3},{7,4},{8,5},{9,6},{10,7},{11,8},{12,9},{13... | collective-permute-start | bytes 36872 | tf_op jit(solution)/shard_map/ppermute | solution.py:16
  127.5 15.5 %collective-permute-start.20 = (f32[3,64,64]{1,2,0:T(8,128)S(1)}, f32[3,64,64]{1,2,0:T(8,128)S(1)}, u32[]{:S(2)}, u32[]{:S(2)}) collective-permute-start(f32[3,64,64]{1,2,0:T(8,128)S(1)} %constant_dynamic-slice_fusion.1), channel_id=1, source_target_pairs={{0,3},{1,4},{2,5},{3,6},{4,7},{5,8},{6,9},{7,10},{8,11},{9,12},{10... | collective-permute-start | bytes 147464 | tf_op jit(solution)/shard_map/ppermute | solution.py:16
  131.6 19.8 %collective-permute-start.22 = (f32[3,64,128]{1,2,0:T(8,128)S(1)}, f32[3,64,128]{1,2,0:T(8,128)S(1)}, u32[]{:S(2)}, u32[]{:S(2)}) collective-permute-start(f32[3,64,128]{1,2,0:T(8,128)S(1)} %get-tuple-element.404), channel_id=1, source_target_pairs={{2,0},{3,1},{4,2},{5,3},{6,4},{7,5},{8,6},{9,7},{10,8},{11,9},{12,... | collective-permute-start | bytes 294920 | tf_op jit(solution)/shard_map/ppermute | solution.py:16
  132.9 18.6 %collective-permute-start.21 = (f32[3,64,128]{1,2,0:T(8,128)S(1)}, f32[3,64,128]{1,2,0:T(8,128)S(1)}, u32[]{:S(2)}, u32[]{:S(2)}) collective-permute-start(f32[3,64,128]{1,2,0:T(8,128)S(1)} %get-tuple-element.404), channel_id=1, source_target_pairs={{1,0},{2,1},{3,2},{4,3},{5,4},{6,5},{7,6},{8,7},{9,8},{10,9},{11,1... | collective-permute-start | bytes 294920 | tf_op jit(solution)/shard_map/ppermute | solution.py:16
  134.2 21.4 %collective-permute-start.19 = (f32[3,64,128]{1,2,0:T(8,128)S(1)}, f32[3,64,128]{1,2,0:T(8,128)S(1)}, u32[]{:S(2)}, u32[]{:S(2)}) collective-permute-start(f32[3,64,128]{1,2,0:T(8,128)S(1)} %get-tuple-element.405), channel_id=1, source_target_pairs={{0,2},{1,3},{2,4},{3,5},{4,6},{5,7},{6,8},{7,9},{8,10},{9,11},{10,... | collective-permute-start | bytes 294920 | tf_op jit(solution)/shard_map/ppermute | solution.py:16
  140.4 16.2 %collective-permute-start.18 = (f32[3,64,128]{1,2,0:T(8,128)S(1)}, f32[3,64,128]{1,2,0:T(8,128)S(1)}, u32[]{:S(2)}, u32[]{:S(2)}) collective-permute-start(f32[3,64,128]{1,2,0:T(8,128)S(1)} %get-tuple-element.405), channel_id=1, source_target_pairs={{0,1},{1,2},{2,3},{3,4},{4,5},{5,6},{6,7},{7,8},{8,9},{9,10},{10,1... | collective-permute-start | bytes 294920 | tf_op jit(solution)/shard_map/ppermute | solution.py:16
  143.0 7.8 %collective-permute-start.23 = (f32[3,64,64]{1,2,0:T(8,128)S(1)}, f32[3,64,64]{1,2,0:T(8,128)S(1)}, u32[]{:S(2)}, u32[]{:S(2)}) collective-permute-start(f32[3,64,64]{1,2,0:T(8,128)S(1)} %slice.1928), channel_id=1, source_target_pairs={{3,0},{4,1},{5,2},{6,3},{7,4},{8,5},{9,6},{10,7},{11,8},{12,9},{13... | collective-permute-start | bytes 147464 | tf_op jit(solution)/shard_map/ppermute | solution.py:16
  151.5 0.9 copy-start.41
  151.5 0.9 copy-start.53
  153.2 0.8 copy-start.37
  153.2 0.8 copy-start.49
  157.3 0.8 copy-start.19
  157.3 0.8 copy-start.33
  164.4 22.2 %collective-permute-start.28 = (f32[3,64,128]{1,2,0:T(8,128)S(1)}, f32[3,64,128]{1,2,0:T(8,128)S(1)}, u32[]{:S(2)}, u32[]{:S(2)}) collective-permute-start(f32[3,64,128]{1,2,0:T(8,128)S(1)} %get-tuple-element.402), channel_id=1, source_target_pairs={{2,0},{3,1},{4,2},{5,3},{6,4},{7,5},{8,6},{9,7},{10,8},{11,9},{12,... | collective-permute-start | bytes 294920 | tf_op jit(solution)/shard_map/ppermute | solution.py:16
  165.7 20.9 %collective-permute-start.27 = (f32[3,64,128]{1,2,0:T(8,128)S(1)}, f32[3,64,128]{1,2,0:T(8,128)S(1)}, u32[]{:S(2)}, u32[]{:S(2)}) collective-permute-start(f32[3,64,128]{1,2,0:T(8,128)S(1)} %get-tuple-element.402), channel_id=1, source_target_pairs={{1,0},{2,1},{3,2},{4,3},{5,4},{6,5},{7,6},{8,7},{9,8},{10,9},{11,1... | collective-permute-start | bytes 294920 | tf_op jit(solution)/shard_map/ppermute | solution.py:16
  167.0 11.0 %collective-permute-start.29 = (f32[3,64,64]{1,2,0:T(8,128)S(1)}, f32[3,64,64]{1,2,0:T(8,128)S(1)}, u32[]{:S(2)}, u32[]{:S(2)}) collective-permute-start(f32[3,64,64]{1,2,0:T(8,128)S(1)} %slice.1959), channel_id=1, source_target_pairs={{3,0},{4,1},{5,2},{6,3},{7,4},{8,5},{9,6},{10,7},{11,8},{12,9},{13... | collective-permute-start | bytes 147464 | tf_op jit(solution)/shard_map/ppermute | solution.py:16
  168.9 21.8 %collective-permute-start.25 = (f32[3,64,128]{1,2,0:T(8,128)S(1)}, f32[3,64,128]{1,2,0:T(8,128)S(1)}, u32[]{:S(2)}, u32[]{:S(2)}) collective-permute-start(f32[3,64,128]{1,2,0:T(8,128)S(1)} %get-tuple-element.403), channel_id=1, source_target_pairs={{0,2},{1,3},{2,4},{3,5},{4,6},{5,7},{6,8},{7,9},{8,10},{9,11},{10,... | collective-permute-start | bytes 294920 | tf_op jit(solution)/shard_map/ppermute | solution.py:16
  174.5 17.2 %collective-permute-start.24 = (f32[3,64,128]{1,2,0:T(8,128)S(1)}, f32[3,64,128]{1,2,0:T(8,128)S(1)}, u32[]{:S(2)}, u32[]{:S(2)}) collective-permute-start(f32[3,64,128]{1,2,0:T(8,128)S(1)} %get-tuple-element.403), channel_id=1, source_target_pairs={{0,1},{1,2},{2,3},{3,4},{4,5},{5,6},{6,7},{7,8},{8,9},{9,10},{10,1... | collective-permute-start | bytes 294920 | tf_op jit(solution)/shard_map/ppermute | solution.py:16
  177.9 8.0 %collective-permute-start.26 = (f32[3,64,64]{1,2,0:T(8,128)}, f32[3,64,64]{1,2,0:T(8,128)S(1)}, u32[]{:S(2)}, u32[]{:S(2)}) collective-permute-start(f32[3,64,64]{1,2,0:T(8,128)} %constant_dynamic-slice_fusion), channel_id=1, source_target_pairs={{0,3},{1,4},{2,5},{3,6},{4,7},{5,8},{6,9},{7,10},{8,11},{9,12},{10... | collective-permute-start | bytes 147464 | tf_op jit(solution)/shard_map/ppermute | solution.py:16
  186.6 0.9 copy-start.42
  186.6 0.9 copy-start.54
  188.4 0.8 copy-start.38
  188.4 0.8 copy-start.50
  (42 other events, 29.7 us)
